TPU v7x, 32 devices: a whole 2x2x4 slice. The times are simulated.
32 devices in a mesh: seq: 8 (over y, x, core), head: 4 (over z).
Axes of the slice: x: 2, y: 2, z: 4, core: 2. Of those that a mesh axis runs over, the one named last changes fastest.
Arguments:
- tokens: bfloat16 [32, 1024, 1024], P('seq'), may hold values from -6 to 6
- w_query: bfloat16 [1024, 1024], P(None, 'head'), may hold values from -1 to 1
- w_key: bfloat16 [1024, 1024], P(None, 'head'), may hold values from -1 to 1
- w_value: bfloat16 [1024, 1024], P(None, 'head'), may hold values from -0.1875 to 0.1875
- w_out: bfloat16 [1024, 1024], P('head'), may hold values from -0.1875 to 0.1875
Outputs:
- mixed: bfloat16 [32, 1024, 1024], P('seq', None, 'head')
All inputs are finite; a program needn't handle non-finite values.
Results may differ from a plain program's by a relative error of at most 0.012.
Values may be sent and summed in bfloat16 or wider, within the bound.
No kernel may reach another device: no remote copies, remote signals or barrier semaphores. Data moves between devices by JAX's collectives and lax.ppermute only.
A program may use at most 128 MiB of HBM per device.

v0:
```python
import jax
import jax.numpy as jnp
from jax import lax
from jax.sharding import PartitionSpec as P

HS = 64
epsilon = 1e-05


def normalize(tokens):
    values = tokens.astype(jnp.float32)
    row_mean = jnp.mean(values, axis=-1, keepdims=True)
    centered = values - row_mean
    row_var = jnp.mean(centered * centered, axis=-1, keepdims=True)
    return (centered * lax.rsqrt(row_var + epsilon)).astype(jnp.bfloat16)


def project(source, weight):
    return jnp.einsum("fpd,dc->fpc", source, weight, preferred_element_type=jnp.float32).astype(
        jnp.bfloat16
    )


def attend(queries, key_rows, value_rows, head_count):
    frames, patch_count, feature_width = queries.shape
    head_size = feature_width // head_count
    query_flat = queries.reshape(frames, patch_count * head_count, head_size)
    key_flat = key_rows.reshape(frames, patch_count * head_count, head_size)
    value_flat = value_rows.reshape(frames, patch_count * head_count, head_size)
    scores = jnp.einsum(
        "fmd,gmd->fgm", query_flat, key_flat, preferred_element_type=jnp.float32
    ) * head_size ** (-0.5)
    row_top = jnp.max(scores, axis=1, keepdims=True)
    raised = jnp.exp(scores - row_top)
    weights = (raised / jnp.sum(raised, axis=1, keepdims=True)).astype(jnp.bfloat16)
    attended = jnp.einsum("fgm,gmd->fmd", weights, value_flat, preferred_element_type=jnp.float32)
    return attended.astype(jnp.bfloat16).reshape(frames, patch_count, feature_width)


def local(tokens, w_query, w_key, w_value, w_out):
    normed = normalize(tokens)
    head_count = w_query.shape[1] // HS
    local_query = project(normed, w_query)
    local_key = project(normed, w_key)
    local_value = project(normed, w_value)
    queries, key_rows, value_rows = (
        lax.all_to_all(local_query, "seq", split_axis=1, concat_axis=0, tiled=True),
        lax.all_to_all(local_key, "seq", split_axis=1, concat_axis=0, tiled=True),
        lax.all_to_all(local_value, "seq", split_axis=1, concat_axis=0, tiled=True),
    )
    attended = attend(queries, key_rows, value_rows, head_count)
    partial_value = jnp.einsum("fpc,cd->fpd", attended, w_out, preferred_element_type=jnp.float32)
    columns = lax.psum_scatter(
        partial_value.astype(jnp.bfloat16), "head", scatter_dimension=2, tiled=True
    )
    return lax.all_to_all(columns, "seq", split_axis=0, concat_axis=1, tiled=True)


def solution(mesh):
    return jax.shard_map(
        local,
        mesh=mesh,
        in_specs=(
            P("seq", None, None),
            P(None, "head"),
            P(None, "head"),
            P(None, "head"),
            P("head", None),
        ),
        out_specs=P("seq", None, "head"),
        check_vma=False,
    )
```

profile of v0, /device:TPU:0, one launch (start us, length us, event | category | flops | bytes accessed | tf_op | source)
XLA Modules:
  0.0 326.3 jit_solution(13314724638309537397)
XLA Ops:
  6.5 4.7 %convert_reduce_fusion = f32[4,1024]{1,0:T(4,128)S(1)} fusion(bf16[4,1024,1024]{2,1,0:T(8,128)(2,1)} %param.5), kind=kLoop, calls=%fused_computation.2 | loop fusion | flops 8384512 | bytes 8404992 | tf_op jit(solution)/shard_map/reduce_sum | solution.py:12
  11.3 1.1 copy-done.1
  12.4 2.8 fusion.3
  15.2 3.1 fusion.28
  18.4 3.0 copy.19
  21.3 5.2 %all-to-all-start.1 = ((bf16[4,1024,256]{2,0,1:T(4,128)(2,1)}), bf16[4,1024,256]{2,0,1:T(4,128)(2,1)S(1)}, u32[]{:S(2)}, u32[]{:S(2)}) async-start(bf16[4,1024,256]{2,0,1:T(4,128)(2,1)} %copy.19), calls=%async_computation.1 | async-start | bytes 4194304 | tf_op jit(solution)/shard_map/all_to_all | solution.py:48
  26.5 5.0 %fusion.31 = bf16[4,1024,256]{2,1,0:T(8,128)(2,1)S(1)} fusion(bf16[4,1024,1024]{2,1,0:T(8,128)(2,1)} %param.5, f32[4,1024]{1,0:T(4,128)S(1)} %add_rsqrt_fusion, f32[4,1024]{1,0:T(4,128)S(1)} %broadcast_multiply_fusion, bf16[1024,256]{1,0:T(8,128)(2,1)S(1)} %copy-done.4), kind=kOutput, calls=%fused_computation.30 | convolution fusion | flops 2165309440 | bytes 11042816 | tf_op jit(solution)/shard_map/fpd,dc->fpc/dot_general | solution.py:19
  31.6 2.9 copy.21
  34.5 18.6 %all-to-all-done.1 = bf16[4,1024,256]{2,0,1:T(4,128)(2,1)S(1)} async-done(((bf16[4,1024,256]{2,0,1:T(4,128)(2,1)}), bf16[4,1024,256]{2,0,1:T(4,128)(2,1)S(1)}, u32[]{:S(2)}, u32[]{:S(2)}) %all-to-all-start.1) | async-done | bytes 2097184 | tf_op jit(solution)/shard_map/all_to_all | solution.py:48
  53.1 4.3 %all-to-all-start.2 = ((bf16[4,1024,256]{2,0,1:T(4,128)(2,1)}), bf16[4,1024,256]{2,0,1:T(4,128)(2,1)}, u32[]{:S(2)}, u32[]{:S(2)}) async-start(bf16[4,1024,256]{2,0,1:T(4,128)(2,1)} %copy.21), calls=%async_computation.2 | async-start | bytes 4194304 | tf_op jit(solution)/shard_map/all_to_all | solution.py:47
  57.5 5.0 %fusion.25 = bf16[4,1024,256]{2,1,0:T(8,128)(2,1)S(1)} fusion(bf16[4,1024,1024]{2,1,0:T(8,128)(2,1)} %param.5, f32[4,1024]{1,0:T(4,128)S(1)} %add_rsqrt_fusion, f32[4,1024]{1,0:T(4,128)S(1)} %broadcast_multiply_fusion, bf16[1024,256]{1,0:T(8,128)(2,1)S(1)} %copy-done.5), kind=kOutput, calls=%fused_computation.28 | convolution fusion | flops 2165309440 | bytes 11042816 | tf_op jit(solution)/shard_map/fpd,dc->fpc/dot_general | solution.py:19
  62.5 2.9 copy.17
  65.5 18.7 %all-to-all-done.2 = bf16[4,1024,256]{2,0,1:T(4,128)(2,1)} async-done(((bf16[4,1024,256]{2,0,1:T(4,128)(2,1)}), bf16[4,1024,256]{2,0,1:T(4,128)(2,1)}, u32[]{:S(2)}, u32[]{:S(2)}) %all-to-all-start.2) | async-done | bytes 2097184 | tf_op jit(solution)/shard_map/all_to_all | solution.py:47
  84.1 4.4 %all-to-all-start = ((bf16[4,1024,256]{2,0,1:T(4,128)(2,1)}), bf16[4,1024,256]{2,0,1:T(4,128)(2,1)}, u32[]{:S(2)}, u32[]{:S(2)}) async-start(bf16[4,1024,256]{2,0,1:T(4,128)(2,1)} %copy.17), calls=%async_computation | async-start | bytes 4194304 | tf_op jit(solution)/shard_map/all_to_all | solution.py:49
  88.5 0.2 reduce-scatter.2.cloned.1.call-start
  88.7 2.0 copy.42
  90.7 3.3 reshape.30
  94.0 2.0 copy.41
  95.9 3.2 reshape.31
  99.2 8.3 %fusion.18 = f32[512,32,32]{2,1,0:T(8,128)S(1)} fusion(bf16[32,512,64]{2,1,0:T(8,128)(2,1)} %reshape.31, bf16[32,512,64]{2,1,0:T(8,128)(2,1)} %reshape.30), kind=kOutput, calls=%fused_computation.19 | convolution fusion | flops 67108864 | bytes 6291456 | tf_op jit(solution)/shard_map/fmd,gmd->fgm/dot_general | solution.py:30
  107.5 6.1 %fusion.39 = (f32[32,512]{0,1:T(8,128)S(1)}, f32[32,32,512]{0,1,2:T(8,128)}) fusion(f32[512,32,32]{2,1,0:T(8,128)S(1)} %fusion.18), kind=kOutput, calls=%fused_computation.38 | output fusion | flops 2097183 | bytes 4259840 | tf_op jit(solution)/shard_map/sub | solution.py:34
  113.6 1.5 all-to-all-done
  115.1 2.0 copy.43
  117.1 3.3 %reshape.29 = bf16[32,512,64]{2,1,0:T(8,128)(2,1)} reshape(bf16[8,4,128,256]{3,2,1,0:T(8,128)(2,1)S(1)} %bitcast.50) | data formatting | bytes 4194304 | tf_op jit(solution)/shard_map/reshape | solution.py:29
  120.4 8.1 %convert_bitcast_fusion = bf16[32,512,64]{2,0,1:T(8,128)(2,1)S(1)} fusion(f32[32,32,512]{0,1,2:T(8,128)} %get-tuple-element.6, f32[32,512]{0,1:T(8,128)S(1)} %get-tuple-element.5, bf16[32,512,64]{2,1,0:T(8,128)(2,1)} %reshape.29), kind=kOutput, calls=%fused_computation.22 | convolution fusion | flops 69206016 | bytes 6356992 | tf_op jit(solution)/shard_map/fgm,gmd->fmd/dot_general | solution.py:36
  128.5 3.6 %copy.27 = bf16[32,512,64]{2,1,0:T(8,128)(2,1)} copy(bf16[32,512,64]{2,0,1:T(8,128)(2,1)S(1)} %convert_bitcast_fusion) | data formatting | bytes 4194304 | tf_op jit(solution)/shard_map/convert_element_type | solution.py:37
  132.1 5.5 %reshape.32 = bf16[32,128,256]{2,1,0:T(8,128)(2,1)S(1)} reshape(bf16[32,512,64]{2,1,0:T(8,128)(2,1)} %copy.27) | data formatting | bytes 4194304 | tf_op jit(solution)/shard_map/reshape | solution.py:37
  137.6 5.6 %convolution_convert_fusion = bf16[32,128,1024]{2,1,0:T(8,128)(2,1)} fusion(bf16[32,128,256]{2,1,0:T(8,128)(2,1)S(1)} %reshape.32, bf16[256,1024]{1,0:T(8,128)(2,1)S(1)} %copy-done), kind=kOutput, calls=%fused_computation.13 | convolution fusion | flops 2151677952 | bytes 11010048 | tf_op jit(solution)/shard_map/fpc,cd->fpd/dot_general | solution.py:52
  143.1 0.0 reduce-scatter.2.cloned.1.call-update
  143.2 144.7 %reduce-scatter.2.cloned.1.call-done = bf16[32,128,256]{2,1,0:T(8,128)(2,1)} async-done(((bf16[32,128,1024]{2,1,0:T(8,128)(2,1)}), bf16[32,128,256]{2,1,0:T(8,128)(2,1)}) %reduce-scatter.2.cloned.1.call-update) | async-done | bytes 2097168 | tf_op jit(solution)/shard_map/reduce_scatter | solution.py:53
  287.8 30.2 %all_to_all.63 = bf16[32,128,256]{2,1,0:T(8,128)(2,1)S(1)} all-to-all(bf16[32,128,256]{2,1,0:T(8,128)(2,1)} %reduce-scatter.2.cloned.1.call-done), channel_id=1, replica_groups=mesh['seq'=8,'head'=4] {'seq'}, dimensions={0} | all-to-all | bytes 4194304 | tf_op jit(solution)/shard_map/all_to_all | solution.py:56
  318.0 1.5 copy.28
  (13 shorter events, 0.0 us)
Async XLA Ops:
  6.5 131.0 %copy-start = (bf16[256,1024]{1,0:T(8,128)(2,1)S(1)}, bf16[256,1024]{1,0:T(8,128)(2,1)}, u32[]{:S(2)}) copy-start(bf16[256,1024]{1,0:T(8,128)(2,1)} %param.9) | copy-start | bytes 1572868
  6.5 5.8 %copy-start.1 = (bf16[4,1024,1024]{2,1,0:T(8,128)(2,1)S(1)}, bf16[4,1024,1024]{2,1,0:T(8,128)(2,1)}, u32[]{:S(2)}) copy-start(bf16[4,1024,1024]{2,1,0:T(8,128)(2,1)} %param.5) | copy-start | bytes 25165828
  6.5 8.6 %copy-start.3 = (bf16[1024,256]{1,0:T(8,128)(2,1)S(1)}, bf16[1024,256]{1,0:T(8,128)(2,1)}, u32[]{:S(2)}) copy-start(bf16[1024,256]{1,0:T(8,128)(2,1)} %param.7) | copy-start | bytes 1572868
  18.3 8.2 %copy-start.4 = (bf16[1024,256]{1,0:T(8,128)(2,1)S(1)}, bf16[1024,256]{1,0:T(8,128)(2,1)}, u32[]{:S(2)}) copy-start(bf16[1024,256]{1,0:T(8,128)(2,1)} %param.6) | copy-start | bytes 1572868
  21.3 31.8 %all-to-all-start.1 = ((bf16[4,1024,256]{2,0,1:T(4,128)(2,1)}), bf16[4,1024,256]{2,0,1:T(4,128)(2,1)S(1)}, u32[]{:S(2)}, u32[]{:S(2)}) async-start(bf16[4,1024,256]{2,0,1:T(4,128)(2,1)} %copy.19), calls=%async_computation.1 | async-start | bytes 4194304 | tf_op jit(solution)/shard_map/all_to_all | solution.py:48
  31.5 25.9 %copy-start.5 = (bf16[1024,256]{1,0:T(8,128)(2,1)S(1)}, bf16[1024,256]{1,0:T(8,128)(2,1)}, u32[]{:S(2)}) copy-start(bf16[1024,256]{1,0:T(8,128)(2,1)} %param.8) | copy-start | bytes 1572868
  53.1 9.4 %copy-start.2 = (bf16[4,1024,256]{2,0,1:T(4,128)(2,1)}, bf16[4,1024,256]{2,0,1:T(4,128)(2,1)S(1)}, u32[]{:S(2)}) copy-start(bf16[4,1024,256]{2,0,1:T(4,128)(2,1)S(1)} %all-to-all-done.1) | copy-start | bytes 6291460
  53.1 31.0 %all-to-all-start.2 = ((bf16[4,1024,256]{2,0,1:T(4,128)(2,1)}), bf16[4,1024,256]{2,0,1:T(4,128)(2,1)}, u32[]{:S(2)}, u32[]{:S(2)}) async-start(bf16[4,1024,256]{2,0,1:T(4,128)(2,1)} %copy.21), calls=%async_computation.2 | async-start | bytes 4194304 | tf_op jit(solution)/shard_map/all_to_all | solution.py:47
  84.1 31.0 %all-to-all-start = ((bf16[4,1024,256]{2,0,1:T(4,128)(2,1)}), bf16[4,1024,256]{2,0,1:T(4,128)(2,1)}, u32[]{:S(2)}, u32[]{:S(2)}) async-start(bf16[4,1024,256]{2,0,1:T(4,128)(2,1)} %copy.17), calls=%async_computation | async-start | bytes 4194304 | tf_op jit(solution)/shard_map/all_to_all | solution.py:49
  88.5 199.3 %reduce-scatter.2.cloned.1.call-start = ((), (), s32[]{:S(2)}) async-start(), calls=%async_computation.5 | async-start | bytes 10485760 | tf_op jit(solution)/shard_map/reduce_scatter | solution.py:53
Sparse Core Ops, SparseCore 0:
  143.3 144.4 reduce-scatter.1
where the time goes:
time: 327 us; the launch traced here: 326 us
  waiting for transfers between devices  184 us (56%)
  local copies, waits for them, and re-layouts  36.1 us (11%)
  matrix products  35.2 us (11%)
  blocking collectives  30.2 us (9%)
  starting transfers between devices  14.1 us (4%)
  other arithmetic  13.6 us (4%)
  between operations  13.6 us (4%)
    reduce_scatter x1, waiting for transfers between devices, local(): lax.psum_scatter(partial_value.astype(jnp.bfloat16), 'head', scatter_dime...  145 us
    all_to_all x1, blocking collectives, local(): lax.all_to_all(columns, 'seq', split_axis=0, concat_axis=1, tiled=True)  30.2 us
    all_to_all x1, waiting for transfers between devices, local(): lax.all_to_all(local_query, 'seq', split_axis=1, concat_axis=0, tiled=True)  18.7 us
    all_to_all x1, waiting for transfers between devices, local(): lax.all_to_all(local_key, 'seq', split_axis=1, concat_axis=0, tiled=True)  18.6 us
    dot_general x3, matrix products, project(): jnp.einsum('fpd,dc->fpc', source, weight, preferred_element_type=jnp.floa...  13.2 us
    convert_element_type x3, local copies, waits for them, and re-layouts, project(): jnp.einsum('fpd,dc->fpc', source, weight, preferred_element_type=jnp.floa...  8.83 us
    dot_general x1, matrix products, attend(): jnp.einsum('fmd,gmd->fgm', query_flat, key_flat, preferred_element_type=j...  8.29 us
    dot_general x1, matrix products, attend(): jnp.einsum('fgm,gmd->fmd', weights, value_flat, preferred_element_type=jn...  8.14 us
  transfers between devices with their start and end apart: 4, of which 4 were waited for; matrix products, arithmetic and copies ran while one was open for 12% of the time, Pallas kernels for 0%

commit v1 on v0

--- a/solution.py
+++ b/solution.py
@@ -5,6 +5,33 @@
 
 HS = 64
 epsilon = 1e-05
+
+
+def measure_members_all_by_axis(arr_in, dim_no, sample):
+    mat_out = arr_in.shape
+    work_now = arr_in.reshape(
+        *mat_out[:dim_no], sample, mat_out[dim_no] // sample, *mat_out[dim_no + 1 :]
+    )
+    return jnp.moveaxis(work_now, dim_no, 0)
+
+
+def process_stops_all(vector, k_dim):
+    vector = jnp.moveaxis(vector, 0, k_dim)
+    mid_arr = vector.shape
+    return vector.reshape(
+        *mid_arr[:k_dim], mid_arr[k_dim] * mid_arr[k_dim + 1], *mid_arr[k_dim + 2 :]
+    )
+
+
+def clear_joints(buf, lane_axis, field_in, my_tile):
+    local_now, wide_out = (lax.psum(1, lane_axis), lax.axis_index(lane_axis))
+    known = measure_members_all_by_axis(buf, field_in, local_now)
+    row_list = [known[wide_out]]
+    for b in range(1, local_now):
+        carry = known[wide_out ^ b]
+        row_list.append(lax.ppermute(carry, lane_axis, [(no, no ^ b) for no in range(local_now)]))
+    known = jnp.stack(row_list, 0)[wide_out ^ jnp.arange(local_now)]
+    return process_stops_all(known, my_tile)
 
 
 def normalize(tokens):
@@ -45,7 +72,7 @@
     local_value = project(normed, w_value)
     queries, key_rows, value_rows = (
         lax.all_to_all(local_query, "seq", split_axis=1, concat_axis=0, tiled=True),
-        lax.all_to_all(local_key, "seq", split_axis=1, concat_axis=0, tiled=True),
+        clear_joints(local_key, "seq", 1, 0),
         lax.all_to_all(local_value, "seq", split_axis=1, concat_axis=0, tiled=True),
     )
     attended = attend(queries, key_rows, value_rows, head_count)

time: 327 us -> 315 us (0.963)
  waiting for transfers between devices: 184 us -> 155 us
  local copies, waits for them, and re-layouts: 36.1 us -> 47 us
    all_to_all x1 -> x0, waiting for transfers between devices: 18.6 us -> none  [local(): lax.all_to_all(local_key, 'seq', split_axis=1, concat_axis=0, tiled=True)]
    all_to_all x1, waiting for transfers between devices: 18.7 us -> 7.12 us  [local(): lax.all_to_all(local_query, 'seq', split_axis=1, concat_axis=0, tiled=True)]
    unnamed x12 -> x19, local copies, waits for them, and re-layouts: 1.13 us -> 9.95 us
    ppermute x0 -> x7, starting transfers between devices: none -> 7.77 us  [clear_joints(): lax.ppermute(carry, lane_axis, [(no, no ^ b) for no in range(local_now)])]
    all_to_all x1 -> x0, starting transfers between devices: 5.21 us -> none  [local(): lax.all_to_all(local_key, 'seq', split_axis=1, concat_axis=0, tiled=True)]
    another operation x0 -> x2, local copies, waits for them, and re-layouts: none -> 4.91 us  [the longest x1 3.26 us: attend(): key_flat = key_rows.reshape(frames, patch_count * head_count, head_size)]
    ppermute x0 -> x7, waiting for transfers between devices: none -> 3.34 us  [clear_joints(): lax.ppermute(carry, lane_axis, [(no, no ^ b) for no in range(local_now)])]
    convert_element_type x3 -> x2, local copies, waits for them, and re-layouts: 8.83 us -> 7.5 us  [project(): jnp.einsum('fpd,dc->fpc', source, weight, preferred_element_type=jnp.floa...]
  transfers between devices with their start and end apart: 4 -> 10, of which waited for: 4 -> 4; matrix products, arithmetic and copies ran while one was open for 12% -> 17% of each run, Pallas kernels for 0% -> 0%
where the time goes in v1:
time: 315 us; the launch traced here: 314 us
  waiting for transfers between devices  155 us (49%)
  local copies, waits for them, and re-layouts  47 us (15%)
  matrix products  38.2 us (12%)
  blocking collectives  30.2 us (10%)
  starting transfers between devices  16.3 us (5%)
  other arithmetic  13.7 us (4%)
  between operations  13.6 us (4%)
    reduce_scatter x1, waiting for transfers between devices, local(): lax.psum_scatter(partial_value.astype(jnp.bfloat16), 'head', scatter_dime...  145 us
    all_to_all x1, blocking collectives, local(): lax.all_to_all(columns, 'seq', split_axis=0, concat_axis=1, tiled=True)  30.2 us
    dot_general x3, matrix products, project(): jnp.einsum('fpd,dc->fpc', source, weight, preferred_element_type=jnp.floa...  16.2 us
    unnamed x19, local copies, waits for them, and re-layouts  9.95 us
    dot_general x1, matrix products, attend(): jnp.einsum('fmd,gmd->fgm', query_flat, key_flat, preferred_element_type=j...  8.29 us
    dot_general x1, matrix products, attend(): jnp.einsum('fgm,gmd->fmd', weights, value_flat, preferred_element_type=jn...  8.14 us
    ppermute x7, starting transfers between devices, clear_joints(): lax.ppermute(carry, lane_axis, [(no, no ^ b) for no in range(local_now)])  7.77 us
    convert_element_type x2, local copies, waits for them, and re-layouts, project(): jnp.einsum('fpd,dc->fpc', source, weight, preferred_element_type=jnp.floa...  7.5 us
  transfers between devices with their start and end apart: 10, of which 4 were waited for; matrix products, arithmetic and copies ran while one was open for 17% of the time, Pallas kernels for 0%

profile of v1, /device:TPU:0, one launch (start us, length us, event | category | flops | bytes accessed | tf_op | source)
XLA Modules:
  0.0 314.2 jit_solution(8882902447370088988)
XLA Ops:
  6.5 4.7 %convert_reduce_fusion = f32[4,1024]{1,0:T(4,128)S(1)} fusion(bf16[4,1024,1024]{2,1,0:T(8,128)(2,1)} %param.5), kind=kLoop, calls=%fused_computation.3 | loop fusion | flops 8384512 | bytes 8404992 | tf_op jit(solution)/shard_map/reduce_sum | solution.py:39
  12.4 2.8 fusion.3
  15.2 5.1 %fusion.28 = bf16[4,1024,256]{2,1,0:T(8,128)(2,1)S(1)} fusion(bf16[4,1024,1024]{2,1,0:T(8,128)(2,1)} %param.5, f32[4,1024]{1,0:T(4,128)S(1)} %add_rsqrt_fusion, f32[4,1024]{1,0:T(4,128)S(1)} %broadcast_multiply_fusion, bf16[1024,256]{1,0:T(8,128)(2,1)S(1)} %copy-done.4), kind=kOutput, calls=%fused_computation.29 | convolution fusion | flops 2165309440 | bytes 11042816 | tf_op jit(solution)/shard_map/fpd,dc->fpc/dot_general | solution.py:46
  22.1 2.5 collective-permute-start.1
  24.7 1.8 collective-permute-start.3
  26.5 5.0 %fusion.31 = bf16[4,1024,256]{2,1,0:T(8,128)(2,1)S(1)} fusion(bf16[4,1024,1024]{2,1,0:T(8,128)(2,1)} %param.5, f32[4,1024]{1,0:T(4,128)S(1)} %add_rsqrt_fusion, f32[4,1024]{1,0:T(4,128)S(1)} %broadcast_multiply_fusion, bf16[1024,256]{1,0:T(8,128)(2,1)S(1)} %copy-done.5), kind=kOutput, calls=%fused_computation.30 | convolution fusion | flops 2165309440 | bytes 11042816 | tf_op jit(solution)/shard_map/fpd,dc->fpc/dot_general | solution.py:46
  31.5 2.9 copy.18
  34.5 4.0 %all-to-all-start.1 = ((bf16[4,1024,256]{2,0,1:T(4,128)(2,1)}), bf16[4,1024,256]{2,0,1:T(4,128)(2,1)S(1)}, u32[]{:S(2)}, u32[]{:S(2)}) async-start(bf16[4,1024,256]{2,0,1:T(4,128)(2,1)} %copy.18), calls=%async_computation.1 | async-start | bytes 4194304 | tf_op jit(solution)/shard_map/all_to_all | solution.py:74
  38.4 6.1 %fusion.25 = bf16[4,1024,256]{2,1,0:T(8,128)(2,1)} fusion(bf16[4,1024,1024]{2,1,0:T(8,128)(2,1)} %param.5, f32[4,1024]{1,0:T(4,128)S(1)} %add_rsqrt_fusion, f32[4,1024]{1,0:T(4,128)S(1)} %broadcast_multiply_fusion, bf16[1024,256]{1,0:T(8,128)(2,1)} %param.8), kind=kOutput, calls=%fused_computation.28 | convolution fusion | flops 2165309440 | bytes 11042816 | tf_op jit(solution)/shard_map/fpd,dc->fpc/dot_general | solution.py:46
  44.5 1.7 bitcast_dynamic-update-slice_fusion.7
  46.2 4.6 %copy.16 = bf16[4,1024,256]{2,0,1:T(4,128)(2,1)} copy(bf16[4,1024,256]{2,1,0:T(8,128)(2,1)} %fusion.25) | data formatting | bytes 4194304 | tf_op jit(solution)/shard_map/convert_element_type | solution.py:46
  50.8 2.9 collective-permute-start.5
  53.7 1.7 bitcast_dynamic-update-slice_fusion.6
  55.4 1.7 bitcast_dynamic-update-slice_fusion.5
  58.5 7.1 %all-to-all-done.1 = bf16[4,1024,256]{2,0,1:T(4,128)(2,1)S(1)} async-done(((bf16[4,1024,256]{2,0,1:T(4,128)(2,1)}), bf16[4,1024,256]{2,0,1:T(4,128)(2,1)S(1)}, u32[]{:S(2)}, u32[]{:S(2)}) %all-to-all-start.1) | async-done | bytes 2097184 | tf_op jit(solution)/shard_map/all_to_all | solution.py:74
  65.6 4.4 %all-to-all-start = ((bf16[4,1024,256]{2,0,1:T(4,128)(2,1)}), bf16[4,1024,256]{2,0,1:T(4,128)(2,1)}, u32[]{:S(2)}, u32[]{:S(2)}) async-start(bf16[4,1024,256]{2,0,1:T(4,128)(2,1)} %copy.16), calls=%async_computation | async-start | bytes 4194304 | tf_op jit(solution)/shard_map/all_to_all | solution.py:76
  71.3 1.7 bitcast_dynamic-update-slice_fusion.1
  73.0 2.9 collective-permute-done.6
  77.6 2.3 gather_fusion
  79.8 3.3 %reshape_reshape.3 = bf16[32,512,64]{2,1,0:T(8,128)(2,1)} reshape(bf16[8,4,128,256]{3,2,1,0:T(8,128)(2,1)S(1)} %gather_fusion) | data formatting | bytes 4194304 | tf_op jit(solution)/shard_map/reshape;reshape | solution.py:55
  83.1 2.0 copy.37
  85.1 3.3 %reshape.61 = bf16[32,512,64]{2,1,0:T(8,128)(2,1)} reshape(bf16[8,4,128,256]{3,2,1,0:T(8,128)(2,1)S(1)} %bitcast.77) | data formatting | bytes 4194304 | tf_op jit(solution)/shard_map/reshape | solution.py:54
  88.3 8.3 %fusion.18 = f32[512,32,32]{2,1,0:T(8,128)S(1)} fusion(bf16[32,512,64]{2,1,0:T(8,128)(2,1)} %reshape.61, bf16[32,512,64]{2,1,0:T(8,128)(2,1)} %reshape_reshape.3), kind=kOutput, calls=%fused_computation.20 | convolution fusion | flops 67108864 | bytes 6291456 | tf_op jit(solution)/shard_map/fmd,gmd->fgm/dot_general | solution.py:57
  96.6 6.1 %fusion.40 = (f32[32,512]{0,1:T(8,128)S(1)}, f32[32,32,512]{0,1,2:T(8,128)}) fusion(f32[512,32,32]{2,1,0:T(8,128)S(1)} %fusion.18), kind=kOutput, calls=%fused_computation.56 | output fusion | flops 2097183 | bytes 4259840 | tf_op jit(solution)/shard_map/sub | solution.py:61
  102.8 2.0 copy.38
  104.8 3.3 %reshape.59 = bf16[32,512,64]{2,1,0:T(8,128)(2,1)} reshape(bf16[8,4,128,256]{3,2,1,0:T(8,128)(2,1)S(1)} %bitcast.78) | data formatting | bytes 4194304 | tf_op jit(solution)/shard_map/reshape | solution.py:56
  108.0 8.1 %convert_bitcast_fusion = bf16[32,512,64]{2,0,1:T(8,128)(2,1)S(1)} fusion(f32[32,32,512]{0,1,2:T(8,128)} %get-tuple-element.13, f32[32,512]{0,1:T(8,128)S(1)} %get-tuple-element.12, bf16[32,512,64]{2,1,0:T(8,128)(2,1)} %reshape.59), kind=kOutput, calls=%fused_computation.23 | convolution fusion | flops 69206016 | bytes 6356992 | tf_op jit(solution)/shard_map/fgm,gmd->fmd/dot_general | solution.py:63
  116.2 3.6 %copy.24 = bf16[32,512,64]{2,1,0:T(8,128)(2,1)} copy(bf16[32,512,64]{2,0,1:T(8,128)(2,1)S(1)} %convert_bitcast_fusion) | data formatting | bytes 4194304 | tf_op jit(solution)/shard_map/convert_element_type | solution.py:64
  119.8 5.5 %reshape.62 = bf16[32,128,256]{2,1,0:T(8,128)(2,1)S(1)} reshape(bf16[32,512,64]{2,1,0:T(8,128)(2,1)} %copy.24) | data formatting | bytes 4194304 | tf_op jit(solution)/shard_map/reshape | solution.py:64
  125.3 5.6 %convolution_convert_fusion = bf16[32,128,1024]{2,1,0:T(8,128)(2,1)} fusion(bf16[32,128,256]{2,1,0:T(8,128)(2,1)S(1)} %reshape.62, bf16[256,1024]{1,0:T(8,128)(2,1)S(1)} %copy-done), kind=kOutput, calls=%fused_computation.14 | convolution fusion | flops 2151677952 | bytes 11010048 | tf_op jit(solution)/shard_map/fpc,cd->fpd/dot_general | solution.py:79
  130.9 144.8 %reduce-scatter.2.cloned.1.call-done = bf16[32,128,256]{2,1,0:T(8,128)(2,1)} async-done(((bf16[32,128,1024]{2,1,0:T(8,128)(2,1)}), bf16[32,128,256]{2,1,0:T(8,128)(2,1)}) %reduce-scatter.2.cloned.1.call-update) | async-done | bytes 2097168 | tf_op jit(solution)/shard_map/reduce_scatter | solution.py:80
  275.7 30.2 %all_to_all.48 = bf16[32,128,256]{2,1,0:T(8,128)(2,1)S(1)} all-to-all(bf16[32,128,256]{2,1,0:T(8,128)(2,1)} %reduce-scatter.2.cloned.1.call-done), channel_id=1, replica_groups=mesh['seq'=8,'head'=4] {'seq'}, dimensions={0} | all-to-all | bytes 4194304 | tf_op jit(solution)/shard_map/all_to_all | solution.py:83
  (35 shorter events, 9.0 us)
Async XLA Ops:
  6.5 118.7 %copy-start = (bf16[256,1024]{1,0:T(8,128)(2,1)S(1)}, bf16[256,1024]{1,0:T(8,128)(2,1)}, u32[]{:S(2)}) copy-start(bf16[256,1024]{1,0:T(8,128)(2,1)} %param.9) | copy-start | bytes 1572868
  6.5 5.8 %copy-start.1 = (bf16[4,1024,1024]{2,1,0:T(8,128)(2,1)S(1)}, bf16[4,1024,1024]{2,1,0:T(8,128)(2,1)}, u32[]{:S(2)}) copy-start(bf16[4,1024,1024]{2,1,0:T(8,128)(2,1)} %param.5) | copy-start | bytes 25165828
  12.4 2.9 copy-start.4
  15.2 11.3 %copy-start.5 = (bf16[1024,256]{1,0:T(8,128)(2,1)S(1)}, bf16[1024,256]{1,0:T(8,128)(2,1)}, u32[]{:S(2)}) copy-start(bf16[1024,256]{1,0:T(8,128)(2,1)} %param.6) | copy-start | bytes 1572868
  20.3 11.2 %copy-start.3 = (bf16[4,1024,256]{2,1,0:T(8,128)(2,1)}, bf16[4,1024,256]{2,1,0:T(8,128)(2,1)S(1)}, u32[]{:S(2)}) copy-start(bf16[4,1024,256]{2,1,0:T(8,128)(2,1)S(1)} %fusion.28) | copy-start | bytes 6291460
  21.6 29.1 %collective-permute-start = (bf16[4,128,256]{2,1,0:T(8,128)(2,1)}, bf16[4,128,256]{2,1,0:T(8,128)(2,1)}, u32[]{:S(2)}, u32[]{:S(2)}) collective-permute-start(bf16[4,128,256]{2,1,0:T(8,128)(2,1)} %get-tuple-element.11), channel_id=1, source_target_pairs={{0,4},{4,0},{8,12},{12,8},{16,20},{20,16},{24,28},{28,24},{1,5},{5... | collective-permute-start | bytes 786440 | tf_op jit(solution)/shard_map/ppermute | solution.py:32
  22.1 33.2 %collective-permute-start.1 = (bf16[4,128,256]{2,1,0:T(8,128)(2,1)}, bf16[4,128,256]{2,1,0:T(8,128)(2,1)}, u32[]{:S(2)}, u32[]{:S(2)}) collective-permute-start(bf16[4,128,256]{2,1,0:T(8,128)(2,1)} %get-tuple-element.10), channel_id=1, source_target_pairs={{0,8},{4,12},{8,0},{12,4},{16,24},{20,28},{24,16},{28,20},{1,9},{5... | collective-permute-start | bytes 786440 | tf_op jit(solution)/shard_map/ppermute | solution.py:32
  24.6 32.4 %collective-permute-start.2 = (bf16[4,128,256]{2,1,0:T(8,128)(2,1)}, bf16[4,128,256]{2,1,0:T(8,128)(2,1)S(1)}, u32[]{:S(2)}, u32[]{:S(2)}) collective-permute-start(bf16[4,128,256]{2,1,0:T(8,128)(2,1)} %get-tuple-element.9), channel_id=1, source_target_pairs={{0,12},{4,8},{8,4},{12,0},{16,28},{20,24},{24,20},{28,16},{1,13},{... | collective-permute-start | bytes 786440 | tf_op jit(solution)/shard_map/ppermute | solution.py:32
  24.7 33.0 %collective-permute-start.3 = (bf16[4,128,256]{2,1,0:T(8,128)(2,1)}, bf16[4,128,256]{2,1,0:T(8,128)(2,1)S(1)}, u32[]{:S(2)}, u32[]{:S(2)}) collective-permute-start(bf16[4,128,256]{2,1,0:T(8,128)(2,1)} %get-tuple-element.8), channel_id=1, source_target_pairs={{0,16},{4,20},{8,24},{12,28},{16,0},{20,4},{24,8},{28,12},{1,17},{... | collective-permute-start | bytes 786440 | tf_op jit(solution)/shard_map/ppermute | solution.py:32
  26.5 43.7 %collective-permute-start.4 = (bf16[4,128,256]{2,1,0:T(8,128)(2,1)}, bf16[4,128,256]{2,1,0:T(8,128)(2,1)S(1)}, u32[]{:S(2)}, u32[]{:S(2)}) collective-permute-start(bf16[4,128,256]{2,1,0:T(8,128)(2,1)} %get-tuple-element.7), channel_id=1, source_target_pairs={{0,20},{4,16},{8,28},{12,24},{16,4},{20,0},{24,12},{28,8},{1,21},{... | collective-permute-start | bytes 786440 | tf_op jit(solution)/shard_map/ppermute | solution.py:32
  34.5 31.1 %all-to-all-start.1 = ((bf16[4,1024,256]{2,0,1:T(4,128)(2,1)}), bf16[4,1024,256]{2,0,1:T(4,128)(2,1)S(1)}, u32[]{:S(2)}, u32[]{:S(2)}) async-start(bf16[4,1024,256]{2,0,1:T(4,128)(2,1)} %copy.18), calls=%async_computation.1 | async-start | bytes 4194304 | tf_op jit(solution)/shard_map/all_to_all | solution.py:74
  50.8 20.6 %collective-permute-start.5 = (bf16[4,128,256]{2,1,0:T(8,128)(2,1)}, bf16[4,128,256]{2,1,0:T(8,128)(2,1)}, u32[]{:S(2)}, u32[]{:S(2)}) collective-permute-start(bf16[4,128,256]{2,1,0:T(8,128)(2,1)} %get-tuple-element.6), channel_id=1, source_target_pairs={{0,24},{4,28},{8,16},{12,20},{16,8},{20,12},{24,0},{28,4},{1,25},{... | collective-permute-start | bytes 786440 | tf_op jit(solution)/shard_map/ppermute | solution.py:32
  55.4 20.5 %collective-permute-start.6 = (bf16[4,128,256]{2,1,0:T(8,128)(2,1)}, bf16[4,128,256]{2,1,0:T(8,128)(2,1)}, u32[]{:S(2)}, u32[]{:S(2)}) collective-permute-start(bf16[4,128,256]{2,1,0:T(8,128)(2,1)} %get-tuple-element.5), channel_id=1, source_target_pairs={{0,28},{4,24},{8,20},{12,16},{16,12},{20,8},{24,4},{28,0},{1,29},{... | collective-permute-start | bytes 786440 | tf_op jit(solution)/shard_map/ppermute | solution.py:32
  65.6 10.3 %copy-start.2 = (bf16[4,1024,256]{2,0,1:T(4,128)(2,1)}, bf16[4,1024,256]{2,0,1:T(4,128)(2,1)S(1)}, u32[]{:S(2)}) copy-start(bf16[4,1024,256]{2,0,1:T(4,128)(2,1)S(1)} %all-to-all-done.1) | copy-start | bytes 6291460
  65.6 37.2 %all-to-all-start = ((bf16[4,1024,256]{2,0,1:T(4,128)(2,1)}), bf16[4,1024,256]{2,0,1:T(4,128)(2,1)}, u32[]{:S(2)}, u32[]{:S(2)}) async-start(bf16[4,1024,256]{2,0,1:T(4,128)(2,1)} %copy.16), calls=%async_computation | async-start | bytes 4194304 | tf_op jit(solution)/shard_map/all_to_all | solution.py:76
  70.0 205.7 %reduce-scatter.2.cloned.1.call-start = ((), (), s32[]{:S(2)}) async-start(), calls=%async_computation.4 | async-start | bytes 10485760 | tf_op jit(solution)/shard_map/reduce_scatter | solution.py:80
Sparse Core Ops, SparseCore 0:
  131.0 144.6 reduce-scatter.1
